TPU v7x, 32 devices: a whole 2x2x4 slice. The times are simulated.
32 devices in a mesh: gx: 4 (over y, x), gy: 2 (over core), gz: 4 (over z).
Axes of the slice: x: 2, y: 2, z: 4, core: 2. Of those that a mesh axis runs over, the one named last changes fastest.
Arguments:
- potential: float32 [240, 120, 512], P('gx', 'gy', 'gz'), may hold values from -6 to 6
- frag_root: int32 [3, 128], P(None, ('gx', 'gy', 'gz')), may hold values from 0 to 511, as said below
Outputs:
- frag_fields: float32 [128, 110592], P(('gx', 'gy', 'gz'))
Inputs may be any that keep to these rules, and one draw needn't show every extreme that they name: `frag_root`: fragment f is held by the device of linear index f // 4 (gx slowest). Along each dimension the box's first cell is the start of a block plus an offset in [-34, B - 34), B being that dimension's cells of one device. Along y and z that block is the holding device's own; along x it is the block of some device with the same gy and gz index, the anchor. Every anchor of a device supplies exactly 1 of its fragments.
All inputs are finite; a program needn't handle non-finite values.
Results may differ from a plain program's by a relative error of at most 0.00007.
Values sent between devices are 32-bit elements; how exact they have to be, the bound alone decides.
A program may use at most 320 MiB of HBM per device.

v0:
```python
import math

import jax
import jax.numpy as jnp
from jax import lax
from jax.experimental import pallas as pl
from jax.experimental.pallas import tpu as pltpu
from jax.sharding import PartitionSpec as P

G = 48
BOX = 68
HALO = 34
HIGH = lax.Precision.HIGH


def shift(array, axis, step):
    devices = lax.axis_size(axis)
    return lax.ppermute(array, axis, [(i, (i + step) % devices) for i in range(devices)])


def placed(start, cells, period, valid):
    place = cells - start[..., None]
    if period:
        place = jnp.mod(place, period)
    inside = jnp.logical_and(place >= 0, place < BOX)
    inside = jnp.logical_and(inside, valid[..., None])
    base = interp_values()
    index = jnp.where(inside, place, BOX)
    hot = (index[..., None, :] == jnp.arange(BOX, dtype=jnp.int32)[:, None]).astype(jnp.float32)
    return jnp.einsum("ax,...xe->...ae", base, hot, precision=lax.Precision.HIGHEST)


def interp_values():
    row_index = jnp.arange(G, dtype=jnp.int32)[:, None]
    col_index = jnp.arange(BOX, dtype=jnp.int32)[None, :]
    offset = row_index * BOX - col_index * G
    period = G * BOX
    summed = jnp.ones((G, BOX), jnp.float32)
    for harmonic in range(1, G // 2):
        phase_angle = jnp.mod(harmonic * offset, period).astype(jnp.float32)
        summed = summed + 2.0 * jnp.cos(2.0 * math.pi / period * phase_angle)
    return summed / BOX


LANES = 128
FOLD = LANES // HALO
STEPS = 4
BF = jnp.bfloat16
F32 = jnp.float32
FAR = -(1 << 20)


def split(value):
    high = value.astype(BF)
    return high, (value - high.astype(F32)).astype(BF)


def pack_kernel(pot, low, high):
    rows, by = pot.shape[1], pot.shape[2]
    lane = lax.broadcasted_iota(jnp.int32, (rows * by, LANES), 1)
    down = jnp.zeros((rows * by, LANES), F32)
    up = down
    for g in range(FOLD):
        v = pot[g].reshape(rows * by, LANES)
        mine = jnp.logical_and(lane >= g * HALO, lane < (g + 1) * HALO)
        down = jnp.where(mine, pltpu.roll(v, ((g + 1) * HALO) % LANES, 1), down)
        up = jnp.where(mine, pltpu.roll(v, g * HALO, 1) if g else v, up)
    low[...] = down.reshape(rows, by, LANES)
    high[...] = up.reshape(rows, by, LANES)


def pack(pot):
    fold, rows, by, bz = pot.shape
    step = rows // STEPS
    spec = pl.BlockSpec((step, by, LANES), lambda i: (i, 0, 0))
    shape = jax.ShapeDtypeStruct((rows, by, LANES), F32)
    return pl.pallas_call(
        pack_kernel,
        grid=(STEPS,),
        in_specs=[pl.BlockSpec((fold, step, by, LANES), lambda i: (0, i, 0, 0))],
        out_specs=[spec, spec],
        out_shape=[shape, shape],
        cost_estimate=pl.CostEstimate(flops=0, bytes_accessed=4 * pot.size * 2, transcendentals=0),
        name="pack_halos",
    )(pot)


def slab_kernel(ny, *refs):
    owns, lows, highs, out = refs[:ny], refs[ny:2 * ny], refs[2 * ny:3 * ny], refs[3 * ny]
    rows, by = owns[0].shape[1], owns[0].shape[2]
    pad = out.shape[2] // (2 * ny)
    half = ny * pad
    lane = lax.broadcasted_iota(jnp.int32, (pad, LANES), 1)
    blank = jnp.zeros((pad - by, LANES), F32)

    def full(v):
        return jnp.concatenate([v, blank], axis=0)

    for c in range(ny):
        for r in range(rows):
            up = full(highs[c][r])
            down = full(lows[c][r])
            for g in range(FOLD):
                first = full(owns[c][g, r])
                a = pltpu.roll(up, (-g * HALO) % LANES, 1) if g else up
                b = pltpu.roll(down, (HALO - g * HALO) % LANES, 1) if g != 1 else down
                second = jnp.where(lane < HALO, a, jnp.where(lane < 2 * HALO, b, 0.0))
                for side, v in ((0, first), (1, second)):
                    h, l = split(v)
                    cols = slice(side * LANES, (side + 1) * LANES)
                    out[g, r, c * pad:(c + 1) * pad, cols] = h
                    out[g, r, half + c * pad:half + (c + 1) * pad, cols] = l


def slabs(owns, lows, highs):
    ny = len(owns)
    fold, rows, by, bz = owns[0].shape
    pad = -(-by // 16) * 16
    step = rows // STEPS
    big = pl.BlockSpec((fold, step, by, LANES), lambda i: (0, i, 0, 0))
    small = pl.BlockSpec((step, by, LANES), lambda i: (i, 0, 0))
    return pl.pallas_call(
        lambda *refs: slab_kernel(ny, *refs),
        grid=(STEPS,),
        in_specs=[big] * ny + [small] * (2 * ny),
        out_specs=pl.BlockSpec((fold, step, 2 * ny * pad, 2 * LANES), lambda i: (0, i, 0, 0)),
        out_shape=jax.ShapeDtypeStruct((fold, rows, 2 * ny * pad, 2 * LANES), BF),
        cost_estimate=pl.CostEstimate(flops=0, bytes_accessed=16 * 1024 * 1024, transcendentals=0),
        name="build_slabs",
    )(*owns, *lows, *highs)


def contract_kernel(bx, yb, my, mz, out, lhs, wz, us):
    k = my.shape[2]
    for p in range(3):
        h, l = split(my[p])
        lhs[p, :G, :k] = h
        lhs[p, :G, k:] = h
        lhs[p, G:, :k] = l
        lhs[p, G:, k:] = jnp.zeros_like(l)
        h, l = split(mz[p])
        wz[p, 0] = h
        wz[p, 1] = l
    nl, nm = HALO // 8, bx // 8

    def row(p, x, s):
        r = jnp.dot(lhs[p], yb[x], preferred_element_type=F32)
        us[:, s, :] = r[:G] + r[G:]

    def finish(p):
        h, l = split(us[...].reshape(G * 8, us.shape[2]))
        dot = lambda a, b: jnp.dot(a, b, preferred_element_type=F32)
        return dot(h, wz[p, 0]) + dot(h, wz[p, 1]) + dot(l, wz[p, 0])

    def store(r, row0):
        for b in range(G):
            out[pl.ds(row0, 8), b * G:(b + 1) * G] = r[8 * b:8 * b + 8]

    def block(i, carry):
        p = (i >= nl).astype(jnp.int32) + (i >= nl + nm).astype(jnp.int32)
        x0 = jnp.where(p == 0, bx - HALO + 8 * i, jnp.where(p == 1, 8 * (i - nl), 8 * (i - nl - nm)))
        for s in range(8):
            row(p, x0 + s, s)
        store(finish(p), pl.multiple_of(8 * i, 8))
        return carry

    blocks = 2 * nl + nm
    lax.fori_loop(0, blocks, block, 0)
    tail = tail_rows(bx)
    for s, (p, x) in enumerate(tail):
        row(p, x, s)
    sub = lax.broadcasted_iota(jnp.int32, (G * 8, G), 0) % 8
    total = jnp.zeros((G * 8, G), F32)
    for p in range(3):
        places = [s for s, t in enumerate(tail) if t[0] == p]
        mine = jnp.logical_and(sub >= places[0], sub <= places[-1])
        total = jnp.where(mine, finish(p), total)
    store(total, 8 * blocks)


def tail_rows(bx):
    nl, nm = HALO // 8 * 8, bx // 8 * 8
    rows = [(0, bx - HALO + x) for x in range(nl, HALO)]
    rows += [(1, x) for x in range(nm, bx)]
    rows += [(2, x) for x in range(nl, HALO)]
    assert len(rows) == 8
    return rows


def row_order(bx):
    nl, nm = HALO // 8 * 8, bx // 8 * 8
    rows = [(0, bx - HALO + x) for x in range(nl)] + [(1, x) for x in range(nm)]
    return rows + [(2, x) for x in range(nl)] + tail_rows(bx)


def contract(bx, yb, my, mz):
    rows = len(row_order(bx))
    k = my.shape[2]
    width = yb.shape[2]
    return pl.pallas_call(
        lambda *refs: contract_kernel(bx, *refs),
        in_specs=[pl.BlockSpec(memory_space=pltpu.VMEM)] * 3,
        out_specs=pl.BlockSpec(memory_space=pltpu.VMEM),
        out_shape=jax.ShapeDtypeStruct((rows, G * G), F32),
        scratch_shapes=[
            pltpu.VMEM((3, 2 * G, 2 * k), BF),
            pltpu.VMEM((3, 2, width, G), BF),
            pltpu.VMEM((G, 8, width), F32),
        ],
        compiler_params=pltpu.CompilerParams(vmem_limit_bytes=40 * 1024 * 1024),
        cost_estimate=pl.CostEstimate(
            flops=6 * 10 ** 9, bytes_accessed=2 * yb.size + 4 * rows * G * G, transcendentals=0),
        name="contract_yz",
    )(yb, my, mz)


def body(potential, frag_root):
    bx, by, bz = potential.shape
    n = lax.axis_size("gx")
    ny = lax.axis_size("gy")
    nz = lax.axis_size("gz")
    ix, iy, iz = lax.axis_index("gx"), lax.axis_index("gy"), lax.axis_index("gz")
    total_x, total_y, total_z = bx * n, by * ny, bz * nz
    slots = frag_root.shape[1]

    folded = potential.reshape(FOLD, bx // FOLD, by, bz)
    low, high = pack(folded)
    low = shift(low, "gz", 1)
    high = shift(high, "gz", -1)
    owns = [folded] + [shift(folded, "gy", -j) for j in range(1, ny)]
    lows = [low] + [shift(low, "gy", -j) for j in range(1, ny)]
    highs = [high] + [shift(high, "gy", -j) for j in range(1, ny)]
    root = jnp.stack([frag_root] + [shift(frag_root, "gx", j) for j in range(1, n)])
    yb = slabs(owns, lows, highs)
    yb = yb.reshape(bx, yb.shape[2], yb.shape[3])

    anchor = jnp.mod(root[:, 0] + HALO, total_x) // bx
    start_y = jnp.mod(root[:, 1] - iy * by, total_y)
    start_z = jnp.mod(root[:, 2] + HALO - iz * bz, total_z)
    pad = -(-by // 16) * 16
    e = jnp.arange(ny * pad, dtype=jnp.int32)
    cells_y = e // pad * by + e % pad
    real_y = e % pad < by
    e = jnp.arange(2 * LANES, dtype=jnp.int32)
    cells_z = jnp.where(e < bz + HALO, e + HALO, jnp.where(e < bz + 2 * HALO, e - bz - HALO, FAR))
    delta = jnp.array([1, 0, -1], jnp.int32)
    hit = anchor[:, None, :] == jnp.mod(ix + delta, n)[None, :, None]
    valid = jnp.any(hit, axis=2)
    pick = lambda v: jnp.sum(jnp.where(hit, v[:, None, :], 0), axis=2)
    my = placed(pick(start_y), cells_y, total_y, valid)
    my = jnp.where(real_y, my, 0.0)
    mz = placed(pick(start_z), cells_z, None, valid).transpose(0, 1, 3, 2)

    order = [j for j in range(n) if j % 2] + [j for j in range(2, n, 2)]
    got = [None] * n
    for j in order:
        got[j] = shift(contract(bx, yb, my[j], mz[j]), "gx", -j)
    got[0] = contract(bx, yb, my[0], mz[0])

    mine = jnp.mod(frag_root[0] + HALO, total_x)
    slab = mine // bx
    rel = mine - slab * bx
    rows = row_order(bx)
    part = jnp.array([p for p, x in rows], jnp.int32)
    ext = jnp.array([x - (bx - HALO) if p == 0 else x + HALO + (p - 1) * bx for p, x in rows], jnp.int32)
    mx = placed(rel, ext, None, jnp.ones((slots,), bool))
    source = jnp.mod(slab[:, None] - ix + part[None, :] - 1, n)
    fields = None
    for j in [0] + order:
        m = jnp.where((source == j)[:, None, :], mx, 0.0).reshape(slots * G, -1)
        term = jnp.dot(m, got[j], precision=HIGH)
        fields = term if fields is None else fields + term
    return fields.reshape(slots, -1)


def solution(mesh):
    return jax.shard_map(
        body,
        mesh=mesh,
        in_specs=(P("gx", "gy", "gz"), P(None, ("gx", "gy", "gz"))),
        out_specs=P(("gx", "gy", "gz"), None),
        check_vma=False,
    )
```

profile of v0, /device:TPU:0, one launch (start us, length us, event | category | flops | bytes accessed | tf_op | source)
XLA Modules:
  0.0 149.8 jit_solution(4958678072504652302)
XLA Ops:
  0.0 3.0 %collective-permute-start.5 = (s32[3,4]{1,0:T(4,128)}, s32[3,4]{1,0:T(4,128)S(1)}, u32[]{:S(2)}, u32[]{:S(2)}) collective-permute-start(s32[3,4]{1,0:T(4,128)} %param.6), channel_id=1, source_target_pairs={{0,8},{8,16},{16,24},{24,0},{1,9},{9,17},{17,25},{25,1},{2,10},{10... | collective-permute-start | bytes 152 | tf_op jit(solution)/shard_map/ppermute | solution.py:18
  3.0 1.0 collective-permute-start.7
  4.1 1.9 %collective-permute-start.6 = (s32[3,4]{1,0:T(4,128)}, s32[3,4]{1,0:T(4,128)S(1)}, u32[]{:S(2)}, u32[]{:S(2)}) collective-permute-start(s32[3,4]{1,0:T(4,128)} %param.6), channel_id=1, source_target_pairs={{0,16},{8,24},{16,0},{24,8},{1,17},{9,25},{17,1},{25,9},{2,18},{10... | collective-permute-start | bytes 152 | tf_op jit(solution)/shard_map/ppermute | solution.py:18
  6.0 0.0 collective-permute-start
  6.0 4.0 %pack_halos.1 = (f32[20,60,128]{2,1,0:T(8,128)}, f32[20,60,128]{2,1,0:T(8,128)}) custom-call(f32[3,20,60,128]{3,2,1,0:T(8,128)} %bitcast.67), custom_call_target="tpu_custom_call" | custom-call | bytes 3686400 | tf_op jit(solution)/shard_map/pack_halos/pallas_call | solution.py:77
  10.0 1.6 %collective-permute-start.1 = (f32[20,60,128]{2,1,0:T(8,128)}, f32[20,60,128]{2,1,0:T(8,128)S(1)}, u32[]{:S(2)}, u32[]{:S(2)}) collective-permute-start(f32[20,60,128]{2,1,0:T(8,128)} %get-tuple-element.7), channel_id=1, source_target_pairs={{0,1},{1,2},{2,3},{3,0},{4,5},{5,6},{6,7},{7,4},{8,9},{9,10},{10,1... | collective-permute-start | bytes 1843208 | tf_op jit(solution)/shard_map/ppermute | solution.py:18
  11.7 0.1 subtract_select_fusion.1
  11.7 0.1 broadcast_compare_fusion.3
  11.8 2.2 %fusion.124 = f32[48,68]{1,0:T(8,128)S(1)} fusion(s32[68]{0:T(128)S(1)} %iota_multiply_fusion, s32[48]{0:T(128)S(1)} %iota_multiply_fusion.1), kind=kLoop, calls=%fused_computation.188 | loop fusion | flops 829056 | bytes 13520 | tf_op jit(solution)/shard_map/div | solution.py:42
  14.1 0.0 collective-permute-done.5
  14.1 2.3 %collective-permute-start.3 = (f32[20,60,128]{2,1,0:T(8,128)}, f32[20,60,128]{2,1,0:T(8,128)S(1)}, u32[]{:S(2)}, u32[]{:S(2)}) collective-permute-start(f32[20,60,128]{2,1,0:T(8,128)} %get-tuple-element.8), channel_id=1, source_target_pairs={{0,3},{1,0},{2,1},{3,2},{4,7},{5,4},{6,5},{7,6},{8,11},{9,8},{10,9... | collective-permute-start | bytes 1843208 | tf_op jit(solution)/shard_map/ppermute | solution.py:18
  16.4 0.0 collective-permute-done.7
  16.4 0.0 collective-permute-done.6
  16.4 0.2 compare_reduce_fusion
  16.6 0.1 copy.11
  16.8 0.3 fusion.228
  17.0 0.1 copy.12
  17.1 0.1 copy.10
  17.2 0.1 and_select_fusion.1
  17.3 0.3 fusion.2
  17.6 12.0 %collective-permute-done.1.refs_2_ = f32[20,60,128]{2,1,0:T(8,128)S(1)} collective-permute-done((f32[20,60,128]{2,1,0:T(8,128)}, f32[20,60,128]{2,1,0:T(8,128)S(1)}, u32[]{:S(2)}, u32[]{:S(2)}) %collective-permute-start.1) | collective-permute-done | bytes 614432 | tf_op jit(solution)/shard_map/ppermute | solution.py:18
  29.6 0.0 collective-permute-start.2
  29.6 13.6 %collective-permute-done.3.refs_4_ = f32[20,60,128]{2,1,0:T(8,128)S(1)} collective-permute-done((f32[20,60,128]{2,1,0:T(8,128)}, f32[20,60,128]{2,1,0:T(8,128)S(1)}, u32[]{:S(2)}, u32[]{:S(2)}) %collective-permute-start.3) | collective-permute-done | bytes 614432 | tf_op jit(solution)/shard_map/ppermute | solution.py:18
  43.2 0.0 collective-permute-start.4
  43.3 0.1 subtract_select_fusion
  43.4 0.9 fusion.4
  44.3 0.1 slice_bitcast_fusion.3
  44.5 0.0 collective-permute-done.2.refs_3_
  44.5 0.9 collective-permute-done.4.refs_5_
  45.3 0.8 copy-done.4
  46.2 0.0 collective-permute-done.refs_1_
  46.2 7.1 %build_slabs.1 = bf16[3,20,256,256]{3,2,1,0:T(8,128)(2,1)} custom-call(f32[3,20,60,128]{3,2,1,0:T(8,128)} %bitcast.68, f32[3,20,60,128]{3,2,1,0:T(8,128)} %collective-permute-done.refs_1_, f32[20,60,128]{2,1,0:T(8,128)} %copy-done.1, f32[20,60,128]{2,1,0:T(8,128)} %copy-done.3, f32[20,60,128]{2,1,0:T(8,128)} %copy-done.2, f32[20,60,128]{2,1,0:T(8,128)} %copy-done.4), custom_call_target="tpu_custom_call" | custom-call | bytes 16777216 | tf_op jit(solution)/shard_map/build_slabs/pallas_call | solution.py:122
  53.3 3.2 %copy-done = bf16[3,20,256,256]{3,2,1,0:T(8,128)(2,1)S(1)} copy-done((bf16[3,20,256,256]{3,2,1,0:T(8,128)(2,1)S(1)}, bf16[3,20,256,256]{3,2,1,0:T(8,128)(2,1)}, u32[]{:S(2)}) %copy-start) | copy-done | bytes 7864344
  56.5 11.3 %contract_yz.5 = f32[128,2304]{1,0:T(8,128)S(1)} custom-call(bf16[60,256,256]{2,1,0:T(8,128)(2,1)S(1)} %bitcast.62, f32[3,48,128]{2,1,0:T(8,128)S(1)} %get-tuple-element.21.refs_1_, f32[3,256,48]{2,1,0:T(8,128)S(1)} %get-tuple-element.16.refs_2_), custom_call_target="tpu_custom_call" | custom-call | flops 6000000000 | bytes 9043968 | tf_op jit(solution)/shard_map/contract_yz/pallas_call | solution.py:200
  67.8 0.6 collective-permute-start.8
  68.3 11.3 %contract_yz.6 = f32[128,2304]{1,0:T(8,128)S(1)} custom-call(bf16[60,256,256]{2,1,0:T(8,128)(2,1)S(1)} %bitcast.63, f32[3,48,128]{2,1,0:T(8,128)S(1)} %get-tuple-element.20.refs_1_, f32[3,256,48]{2,1,0:T(8,128)S(1)} %get-tuple-element.15.refs_2_), custom_call_target="tpu_custom_call" | custom-call | flops 6000000000 | bytes 9043968 | tf_op jit(solution)/shard_map/contract_yz/pallas_call | solution.py:200
  79.6 1.7 %collective-permute-start.9 = (f32[128,2304]{1,0:T(8,128)S(1)}, f32[128,2304]{1,0:T(8,128)S(1)}, u32[]{:S(2)}, u32[]{:S(2)}) collective-permute-start(f32[128,2304]{1,0:T(8,128)S(1)} %contract_yz.6), channel_id=1, source_target_pairs={{0,8},{8,16},{16,24},{24,0},{1,9},{9,17},{17,25},{25,1},{2,10},{10... | collective-permute-start | bytes 3538952 | tf_op jit(solution)/shard_map/ppermute | solution.py:18
  81.3 11.3 %contract_yz.7 = f32[128,2304]{1,0:T(8,128)S(1)} custom-call(bf16[60,256,256]{2,1,0:T(8,128)(2,1)S(1)} %bitcast.64, f32[3,48,128]{2,1,0:T(8,128)S(1)} %get-tuple-element.19.refs_1_, f32[3,256,48]{2,1,0:T(8,128)S(1)} %get-tuple-element.17.refs_2_), custom_call_target="tpu_custom_call" | custom-call | flops 6000000000 | bytes 9043968 | tf_op jit(solution)/shard_map/contract_yz/pallas_call | solution.py:200
  92.6 0.6 collective-permute-start.10
  93.2 0.2 broadcast_select_fusion.3
  93.4 11.3 %contract_yz.4 = f32[128,2304]{1,0:T(8,128)S(1)} custom-call(bf16[60,256,256]{2,1,0:T(8,128)(2,1)S(1)} %bitcast.65, f32[3,48,128]{2,1,0:T(8,128)S(1)} %get-tuple-element.18.refs_1_, f32[3,256,48]{2,1,0:T(8,128)S(1)} %get-tuple-element.14.refs_2_), custom_call_target="tpu_custom_call" | custom-call | flops 6000000000 | bytes 9043968 | tf_op jit(solution)/shard_map/contract_yz/pallas_call | solution.py:200
  104.7 0.9 fusion.240
  105.6 15.9 %collective-permute-done.9 = f32[128,2304]{1,0:T(8,128)S(1)} collective-permute-done((f32[128,2304]{1,0:T(8,128)S(1)}, f32[128,2304]{1,0:T(8,128)S(1)}, u32[]{:S(2)}, u32[]{:S(2)}) %collective-permute-start.9) | collective-permute-done | bytes 1179680 | tf_op jit(solution)/shard_map/ppermute | solution.py:18
  121.4 0.9 fusion.241
  122.4 23.4 %collective-permute-done.10 = f32[128,2304]{1,0:T(8,128)S(1)} collective-permute-done((f32[128,2304]{1,0:T(8,128)S(1)}, f32[128,2304]{1,0:T(8,128)S(1)}, u32[]{:S(2)}, u32[]{:S(2)}) %collective-permute-start.10) | collective-permute-done | bytes 1179680 | tf_op jit(solution)/shard_map/ppermute | solution.py:18
  145.7 0.9 fusion.242
  146.6 1.2 fusion.1
  147.7 2.1 %reshape.249 = f32[4,110592]{1,0:T(4,128)} reshape(f32[192,2304]{1,0:T(8,128)S(1)} %fusion.1) | data formatting | bytes 3538944 | tf_op jit(solution)/shard_map/reshape | solution.py:273
  (27 shorter events, 0.2 us)
Async XLA Ops:
  0.0 11.6 %copy-start.8 = (s32[3]{0:T(128)S(1)}, s32[3]{0:T(128)}, u32[]{:S(2)}) copy-start(s32[3]{0:T(128)} %constant.436.clone) | copy-start | bytes 40
  0.0 11.7 %copy-start.7 = (s32[128]{0:T(128)S(1)}, s32[128]{0:T(128)}, u32[]{:S(2)}) copy-start(s32[128]{0:T(128)} %constant.438.clone) | copy-start | bytes 1540
  0.0 11.7 %copy-start.6 = (s32[128]{0:T(128)S(1)}, s32[128]{0:T(128)}, u32[]{:S(2)}) copy-start(s32[128]{0:T(128)} %constant.437.clone) | copy-start | bytes 1540
  0.0 11.6 %copy-start.5 = (s32[3,4]{1,0:T(4,128)S(1)}, s32[3,4]{1,0:T(4,128)}, u32[]{:S(2)}) copy-start(s32[3,4]{1,0:T(4,128)} %param.6) | copy-start | bytes 148
  0.0 14.1 %collective-permute-start.5 = (s32[3,4]{1,0:T(4,128)}, s32[3,4]{1,0:T(4,128)S(1)}, u32[]{:S(2)}, u32[]{:S(2)}) collective-permute-start(s32[3,4]{1,0:T(4,128)} %param.6), channel_id=1, source_target_pairs={{0,8},{8,16},{16,24},{24,0},{1,9},{9,17},{17,25},{25,1},{2,10},{10... | collective-permute-start | bytes 152 | tf_op jit(solution)/shard_map/ppermute | solution.py:18
  3.0 13.3 %collective-permute-start.7 = (s32[3,4]{1,0:T(4,128)}, s32[3,4]{1,0:T(4,128)S(1)}, u32[]{:S(2)}, u32[]{:S(2)}) collective-permute-start(s32[3,4]{1,0:T(4,128)} %param.6), channel_id=1, source_target_pairs={{0,24},{8,0},{16,8},{24,16},{1,25},{9,1},{17,9},{25,17},{2,26},{10... | collective-permute-start | bytes 152 | tf_op jit(solution)/shard_map/ppermute | solution.py:18
  4.1 12.3 %collective-permute-start.6 = (s32[3,4]{1,0:T(4,128)}, s32[3,4]{1,0:T(4,128)S(1)}, u32[]{:S(2)}, u32[]{:S(2)}) collective-permute-start(s32[3,4]{1,0:T(4,128)} %param.6), channel_id=1, source_target_pairs={{0,16},{8,24},{16,0},{24,8},{1,17},{9,25},{17,1},{25,9},{2,18},{10... | collective-permute-start | bytes 152 | tf_op jit(solution)/shard_map/ppermute | solution.py:18
  6.0 40.2 %collective-permute-start = (f32[3,20,60,128]{3,2,1,0:T(8,128)}, f32[3,20,60,128]{3,2,1,0:T(8,128)}, u32[]{:S(2)}, u32[]{:S(2)}) collective-permute-start(f32[3,20,60,128]{3,2,1,0:T(8,128)} %bitcast.66), channel_id=1, source_target_pairs={{0,4},{4,0},{1,5},{5,1},{2,6},{6,2},{3,7},{7,3},{8,12},{12,8},{9,1... | collective-permute-start | bytes 5529608 | tf_op jit(solution)/shard_map/ppermute | solution.py:18
  10.0 19.7 %collective-permute-start.1 = (f32[20,60,128]{2,1,0:T(8,128)}, f32[20,60,128]{2,1,0:T(8,128)S(1)}, u32[]{:S(2)}, u32[]{:S(2)}) collective-permute-start(f32[20,60,128]{2,1,0:T(8,128)} %get-tuple-element.7), channel_id=1, source_target_pairs={{0,1},{1,2},{2,3},{3,0},{4,5},{5,6},{6,7},{7,4},{8,9},{9,10},{10,1... | collective-permute-start | bytes 1843208 | tf_op jit(solution)/shard_map/ppermute | solution.py:18
  14.1 29.2 %collective-permute-start.3 = (f32[20,60,128]{2,1,0:T(8,128)}, f32[20,60,128]{2,1,0:T(8,128)S(1)}, u32[]{:S(2)}, u32[]{:S(2)}) collective-permute-start(f32[20,60,128]{2,1,0:T(8,128)} %get-tuple-element.8), channel_id=1, source_target_pairs={{0,3},{1,0},{2,1},{3,2},{4,7},{5,4},{6,5},{7,6},{8,11},{9,8},{10,9... | collective-permute-start | bytes 1843208 | tf_op jit(solution)/shard_map/ppermute | solution.py:18
  29.6 14.8 %copy-start.1 = (f32[20,60,128]{2,1,0:T(8,128)}, f32[20,60,128]{2,1,0:T(8,128)S(1)}, u32[]{:S(2)}) copy-start(f32[20,60,128]{2,1,0:T(8,128)S(1)} %collective-permute-done.1.refs_2_) | copy-start | bytes 1843204
  29.6 14.8 %collective-permute-start.2 = (f32[20,60,128]{2,1,0:T(8,128)S(1)}, f32[20,60,128]{2,1,0:T(8,128)S(1)}, u32[]{:S(2)}, u32[]{:S(2)}) collective-permute-start(f32[20,60,128]{2,1,0:T(8,128)S(1)} %collective-permute-done.1.refs_2_), channel_id=1, source_target_pairs={{0,4},{4,0},{1,5},{5,1},{2,6},{6,2},{3,7},{7,3},{8,12},{12,8},{9,1... | collective-permute-start | bytes 1843208 | tf_op jit(solution)/shard_map/ppermute | solution.py:18
  43.2 1.2 copy-start.2
  43.2 2.1 %collective-permute-start.4 = (f32[20,60,128]{2,1,0:T(8,128)S(1)}, f32[20,60,128]{2,1,0:T(8,128)S(1)}, u32[]{:S(2)}, u32[]{:S(2)}) collective-permute-start(f32[20,60,128]{2,1,0:T(8,128)S(1)} %collective-permute-done.3.refs_4_), channel_id=1, source_target_pairs={{0,4},{4,0},{1,5},{5,1},{2,6},{6,2},{3,7},{7,3},{8,12},{12,8},{9,1... | collective-permute-start | bytes 1843208 | tf_op jit(solution)/shard_map/ppermute | solution.py:18
  44.5 0.9 copy-start.3
  45.3 0.8 copy-start.4
  53.3 3.2 %copy-start = (bf16[3,20,256,256]{3,2,1,0:T(8,128)(2,1)S(1)}, bf16[3,20,256,256]{3,2,1,0:T(8,128)(2,1)}, u32[]{:S(2)}) copy-start(bf16[3,20,256,256]{3,2,1,0:T(8,128)(2,1)} %build_slabs.1) | copy-start | bytes 23592964
  67.8 36.9 %collective-permute-start.8 = (f32[128,2304]{1,0:T(8,128)S(1)}, f32[128,2304]{1,0:T(8,128)S(1)}, u32[]{:S(2)}, u32[]{:S(2)}) collective-permute-start(f32[128,2304]{1,0:T(8,128)S(1)} %contract_yz.5), channel_id=1, source_target_pairs={{0,24},{8,0},{16,8},{24,16},{1,25},{9,1},{17,9},{25,17},{2,26},{10... | collective-permute-start | bytes 3538952 | tf_op jit(solution)/shard_map/ppermute | solution.py:18
  79.6 41.8 %collective-permute-start.9 = (f32[128,2304]{1,0:T(8,128)S(1)}, f32[128,2304]{1,0:T(8,128)S(1)}, u32[]{:S(2)}, u32[]{:S(2)}) collective-permute-start(f32[128,2304]{1,0:T(8,128)S(1)} %contract_yz.6), channel_id=1, source_target_pairs={{0,8},{8,16},{16,24},{24,0},{1,9},{9,17},{17,25},{25,1},{2,10},{10... | collective-permute-start | bytes 3538952 | tf_op jit(solution)/shard_map/ppermute | solution.py:18
  92.6 53.1 %collective-permute-start.10 = (f32[128,2304]{1,0:T(8,128)S(1)}, f32[128,2304]{1,0:T(8,128)S(1)}, u32[]{:S(2)}, u32[]{:S(2)}) collective-permute-start(f32[128,2304]{1,0:T(8,128)S(1)} %contract_yz.7), channel_id=1, source_target_pairs={{0,16},{8,24},{16,0},{24,8},{1,17},{9,25},{17,1},{25,9},{2,18},{10... | collective-permute-start | bytes 3538952 | tf_op jit(solution)/shard_map/ppermute | solution.py:18
where the time goes:
time: 150 us
  waiting for transfers between devices  65.7 us (44%)
  Pallas kernels  56.1 us (37%)
  starting transfers between devices  12.8 us (9%)
  local copies, waits for them, and re-layouts  6.6 us (4%)
  matrix products  5.25 us (4%)
  other arithmetic  3.12 us (2%)
    ppermute x11, waiting for transfers between devices, shift(): lax.ppermute(array, axis, [(i, (i + step) % devices) for i in range(devic...  65.7 us
    pallas_call x4, Pallas kernels, contract(): pl.pallas_call(lambda *refs: contract_kernel(bx, *refs), in_specs=[pl.Blo...  45.1 us
    ppermute x11, starting transfers between devices, shift(): lax.ppermute(array, axis, [(i, (i + step) % devices) for i in range(devic...  12.8 us
    pallas_call x1, Pallas kernels, slabs(): pl.pallas_call(lambda *refs: slab_kernel(ny, *refs), grid=(STEPS,), in_sp...  7.08 us
    unnamed x18, local copies, waits for them, and re-layouts  4.08 us
    pallas_call x1, Pallas kernels, pack(): pl.pallas_call(pack_kernel, grid=(STEPS,), in_specs=[pl.BlockSpec((fold,...  3.99 us
    dot_general x4, matrix products, body(): term = jnp.dot(m, got[j], precision=HIGH)  3.8 us
  transfers between devices with their start and end apart: 11, of which 5 were waited for; matrix products, arithmetic and copies ran while one was open for 5% of the time, Pallas kernels for 25%

commit v1 on v0

--- a/solution.py
+++ b/solution.py
@@ -251,7 +251,7 @@
     my = jnp.where(real_y, my, 0.0)
     mz = placed(pick(start_z), cells_z, None, valid).transpose(0, 1, 3, 2)
 
-    order = [j for j in range(n) if j % 2] + [j for j in range(2, n, 2)]
+    order = [j for j in range(2, n, 2)] + [j for j in range(n) if j % 2]
     got = [None] * n
     for j in order:
         got[j] = shift(contract(bx, yb, my[j], mz[j]), "gx", -j)

time: 150 us -> 138 us (0.920)
  waiting for transfers between devices: 65.7 us -> 53.9 us
    ppermute x11, waiting for transfers between devices: 65.7 us -> 53.9 us  [shift(): lax.ppermute(array, axis, [(i, (i + step) % devices) for i in range(devic...]
  transfers between devices with their start and end apart: 11 -> 11, of which waited for: 5 -> 5; matrix products, arithmetic and copies ran while one was open for 5% -> 5% of each run, Pallas kernels for 25% -> 27%
where the time goes in v1:
time: 138 us
  Pallas kernels  56.1 us (41%)
  waiting for transfers between devices  53.9 us (39%)
  starting transfers between devices  12.8 us (9%)
  local copies, waits for them, and re-layouts  6.6 us (5%)
  matrix products  5.25 us (4%)
  other arithmetic  3.12 us (2%)
    ppermute x11, waiting for transfers between devices, shift(): lax.ppermute(array, axis, [(i, (i + step) % devices) for i in range(devic...  53.9 us
    pallas_call x4, Pallas kernels, contract(): pl.pallas_call(lambda *refs: contract_kernel(bx, *refs), in_specs=[pl.Blo...  45.1 us
    ppermute x11, starting transfers between devices, shift(): lax.ppermute(array, axis, [(i, (i + step) % devices) for i in range(devic...  12.8 us
    pallas_call x1, Pallas kernels, slabs(): pl.pallas_call(lambda *refs: slab_kernel(ny, *refs), grid=(STEPS,), in_sp...  7.08 us
    unnamed x18, local copies, waits for them, and re-layouts  4.08 us
    pallas_call x1, Pallas kernels, pack(): pl.pallas_call(pack_kernel, grid=(STEPS,), in_specs=[pl.BlockSpec((fold,...  3.99 us
    dot_general x4, matrix products, body(): term = jnp.dot(m, got[j], precision=HIGH)  3.79 us
  transfers between devices with their start and end apart: 11, of which 5 were waited for; matrix products, arithmetic and copies ran while one was open for 5% of the time, Pallas kernels for 27%

profile of v1, /device:TPU:0, one launch (start us, length us, event | category | flops | bytes accessed | tf_op | source)
XLA Modules:
  0.0 138.0 jit_solution(849155628178688133)
XLA Ops:
  0.0 3.0 %collective-permute-start.5 = (s32[3,4]{1,0:T(4,128)}, s32[3,4]{1,0:T(4,128)S(1)}, u32[]{:S(2)}, u32[]{:S(2)}) collective-permute-start(s32[3,4]{1,0:T(4,128)} %param.6), channel_id=1, source_target_pairs={{0,8},{8,16},{16,24},{24,0},{1,9},{9,17},{17,25},{25,1},{2,10},{10... | collective-permute-start | bytes 152 | tf_op jit(solution)/shard_map/ppermute | solution.py:18
  3.0 1.0 collective-permute-start.7
  4.1 1.9 %collective-permute-start.6 = (s32[3,4]{1,0:T(4,128)}, s32[3,4]{1,0:T(4,128)S(1)}, u32[]{:S(2)}, u32[]{:S(2)}) collective-permute-start(s32[3,4]{1,0:T(4,128)} %param.6), channel_id=1, source_target_pairs={{0,16},{8,24},{16,0},{24,8},{1,17},{9,25},{17,1},{25,9},{2,18},{10... | collective-permute-start | bytes 152 | tf_op jit(solution)/shard_map/ppermute | solution.py:18
  6.0 0.0 collective-permute-start
  6.0 4.0 %pack_halos.1 = (f32[20,60,128]{2,1,0:T(8,128)}, f32[20,60,128]{2,1,0:T(8,128)}) custom-call(f32[3,20,60,128]{3,2,1,0:T(8,128)} %bitcast.67), custom_call_target="tpu_custom_call" | custom-call | bytes 3686400 | tf_op jit(solution)/shard_map/pack_halos/pallas_call | solution.py:77
  10.0 1.6 %collective-permute-start.1 = (f32[20,60,128]{2,1,0:T(8,128)}, f32[20,60,128]{2,1,0:T(8,128)S(1)}, u32[]{:S(2)}, u32[]{:S(2)}) collective-permute-start(f32[20,60,128]{2,1,0:T(8,128)} %get-tuple-element.7), channel_id=1, source_target_pairs={{0,1},{1,2},{2,3},{3,0},{4,5},{5,6},{6,7},{7,4},{8,9},{9,10},{10,1... | collective-permute-start | bytes 1843208 | tf_op jit(solution)/shard_map/ppermute | solution.py:18
  11.7 0.1 subtract_select_fusion.1
  11.7 0.1 broadcast_compare_fusion.3
  11.8 2.2 %fusion.124 = f32[48,68]{1,0:T(8,128)S(1)} fusion(s32[68]{0:T(128)S(1)} %iota_multiply_fusion, s32[48]{0:T(128)S(1)} %iota_multiply_fusion.1), kind=kLoop, calls=%fused_computation.188 | loop fusion | flops 829056 | bytes 13520 | tf_op jit(solution)/shard_map/div | solution.py:42
  14.1 0.0 collective-permute-done.5
  14.1 2.3 %collective-permute-start.3 = (f32[20,60,128]{2,1,0:T(8,128)}, f32[20,60,128]{2,1,0:T(8,128)S(1)}, u32[]{:S(2)}, u32[]{:S(2)}) collective-permute-start(f32[20,60,128]{2,1,0:T(8,128)} %get-tuple-element.8), channel_id=1, source_target_pairs={{0,3},{1,0},{2,1},{3,2},{4,7},{5,4},{6,5},{7,6},{8,11},{9,8},{10,9... | collective-permute-start | bytes 1843208 | tf_op jit(solution)/shard_map/ppermute | solution.py:18
  16.4 0.0 collective-permute-done.7
  16.4 0.0 collective-permute-done.6
  16.4 0.2 compare_reduce_fusion
  16.6 0.1 copy.11
  16.8 0.3 fusion.228
  17.0 0.1 copy.12
  17.1 0.1 copy.10
  17.2 0.1 and_select_fusion.1
  17.3 0.3 fusion.2
  17.6 12.0 %collective-permute-done.1.refs_2_ = f32[20,60,128]{2,1,0:T(8,128)S(1)} collective-permute-done((f32[20,60,128]{2,1,0:T(8,128)}, f32[20,60,128]{2,1,0:T(8,128)S(1)}, u32[]{:S(2)}, u32[]{:S(2)}) %collective-permute-start.1) | collective-permute-done | bytes 614432 | tf_op jit(solution)/shard_map/ppermute | solution.py:18
  29.6 0.0 collective-permute-start.2
  29.6 13.6 %collective-permute-done.3.refs_4_ = f32[20,60,128]{2,1,0:T(8,128)S(1)} collective-permute-done((f32[20,60,128]{2,1,0:T(8,128)}, f32[20,60,128]{2,1,0:T(8,128)S(1)}, u32[]{:S(2)}, u32[]{:S(2)}) %collective-permute-start.3) | collective-permute-done | bytes 614432 | tf_op jit(solution)/shard_map/ppermute | solution.py:18
  43.2 0.0 collective-permute-start.4
  43.3 0.1 subtract_select_fusion
  43.4 0.9 fusion.4
  44.3 0.1 slice_bitcast_fusion.3
  44.5 0.9 collective-permute-done.4.refs_5_
  45.3 0.8 copy-done.4
  46.2 0.0 collective-permute-done.refs_1_
  46.2 7.1 %build_slabs.1 = bf16[3,20,256,256]{3,2,1,0:T(8,128)(2,1)} custom-call(f32[3,20,60,128]{3,2,1,0:T(8,128)} %bitcast.68, f32[3,20,60,128]{3,2,1,0:T(8,128)} %collective-permute-done.refs_1_, f32[20,60,128]{2,1,0:T(8,128)} %copy-done.1, f32[20,60,128]{2,1,0:T(8,128)} %copy-done.3, f32[20,60,128]{2,1,0:T(8,128)} %copy-done.2, f32[20,60,128]{2,1,0:T(8,128)} %copy-done.4), custom_call_target="tpu_custom_call" | custom-call | bytes 16777216 | tf_op jit(solution)/shard_map/build_slabs/pallas_call | solution.py:122
  53.3 3.2 %copy-done = bf16[3,20,256,256]{3,2,1,0:T(8,128)(2,1)S(1)} copy-done((bf16[3,20,256,256]{3,2,1,0:T(8,128)(2,1)S(1)}, bf16[3,20,256,256]{3,2,1,0:T(8,128)(2,1)}, u32[]{:S(2)}) %copy-start) | copy-done | bytes 7864344
  56.5 11.3 %contract_yz.5 = f32[128,2304]{1,0:T(8,128)S(1)} custom-call(bf16[60,256,256]{2,1,0:T(8,128)(2,1)S(1)} %bitcast.62, f32[3,48,128]{2,1,0:T(8,128)S(1)} %get-tuple-element.21.refs_1_, f32[3,256,48]{2,1,0:T(8,128)S(1)} %get-tuple-element.16.refs_2_), custom_call_target="tpu_custom_call" | custom-call | flops 6000000000 | bytes 9043968 | tf_op jit(solution)/shard_map/contract_yz/pallas_call | solution.py:200
  67.8 0.6 collective-permute-start.8
  68.3 11.3 %contract_yz.6 = f32[128,2304]{1,0:T(8,128)S(1)} custom-call(bf16[60,256,256]{2,1,0:T(8,128)(2,1)S(1)} %bitcast.63, f32[3,48,128]{2,1,0:T(8,128)S(1)} %get-tuple-element.20.refs_1_, f32[3,256,48]{2,1,0:T(8,128)S(1)} %get-tuple-element.15.refs_2_), custom_call_target="tpu_custom_call" | custom-call | flops 6000000000 | bytes 9043968 | tf_op jit(solution)/shard_map/contract_yz/pallas_call | solution.py:200
  79.6 1.6 %collective-permute-start.9 = (f32[128,2304]{1,0:T(8,128)S(1)}, f32[128,2304]{1,0:T(8,128)S(1)}, u32[]{:S(2)}, u32[]{:S(2)}) collective-permute-start(f32[128,2304]{1,0:T(8,128)S(1)} %contract_yz.6), channel_id=1, source_target_pairs={{0,24},{8,0},{16,8},{24,16},{1,25},{9,1},{17,9},{25,17},{2,26},{10... | collective-permute-start | bytes 3538952 | tf_op jit(solution)/shard_map/ppermute | solution.py:18
  81.2 11.3 %contract_yz.7 = f32[128,2304]{1,0:T(8,128)S(1)} custom-call(bf16[60,256,256]{2,1,0:T(8,128)(2,1)S(1)} %bitcast.64, f32[3,48,128]{2,1,0:T(8,128)S(1)} %get-tuple-element.19.refs_1_, f32[3,256,48]{2,1,0:T(8,128)S(1)} %get-tuple-element.17.refs_2_), custom_call_target="tpu_custom_call" | custom-call | flops 6000000000 | bytes 9043968 | tf_op jit(solution)/shard_map/contract_yz/pallas_call | solution.py:200
  92.5 0.7 collective-permute-start.10
  93.2 0.2 broadcast_select_fusion.3
  93.4 11.3 %contract_yz.4 = f32[128,2304]{1,0:T(8,128)S(1)} custom-call(bf16[60,256,256]{2,1,0:T(8,128)(2,1)S(1)} %bitcast.65, f32[3,48,128]{2,1,0:T(8,128)S(1)} %get-tuple-element.18.refs_1_, f32[3,256,48]{2,1,0:T(8,128)S(1)} %get-tuple-element.14.refs_2_), custom_call_target="tpu_custom_call" | custom-call | flops 6000000000 | bytes 9043968 | tf_op jit(solution)/shard_map/contract_yz/pallas_call | solution.py:200
  104.7 0.0 collective-permute-done.8
  104.7 0.9 fusion.240
  105.6 2.9 %collective-permute-done.9 = f32[128,2304]{1,0:T(8,128)S(1)} collective-permute-done((f32[128,2304]{1,0:T(8,128)S(1)}, f32[128,2304]{1,0:T(8,128)S(1)}, u32[]{:S(2)}, u32[]{:S(2)}) %collective-permute-start.9) | collective-permute-done | bytes 1179680 | tf_op jit(solution)/shard_map/ppermute | solution.py:18
  108.5 0.9 fusion.241
  109.4 24.5 %collective-permute-done.10 = f32[128,2304]{1,0:T(8,128)S(1)} collective-permute-done((f32[128,2304]{1,0:T(8,128)S(1)}, f32[128,2304]{1,0:T(8,128)S(1)}, u32[]{:S(2)}, u32[]{:S(2)}) %collective-permute-start.10) | collective-permute-done | bytes 1179680 | tf_op jit(solution)/shard_map/ppermute | solution.py:18
  133.9 0.9 fusion.242
  134.8 1.1 fusion.1
  135.9 2.1 %reshape.249 = f32[4,110592]{1,0:T(4,128)} reshape(f32[192,2304]{1,0:T(8,128)S(1)} %fusion.1) | data formatting | bytes 3538944 | tf_op jit(solution)/shard_map/reshape | solution.py:273
  (27 shorter events, 0.2 us)
Async XLA Ops:
  0.0 11.6 %copy-start.8 = (s32[3]{0:T(128)S(1)}, s32[3]{0:T(128)}, u32[]{:S(2)}) copy-start(s32[3]{0:T(128)} %constant.436.clone) | copy-start | bytes 40
  0.0 11.7 %copy-start.7 = (s32[128]{0:T(128)S(1)}, s32[128]{0:T(128)}, u32[]{:S(2)}) copy-start(s32[128]{0:T(128)} %constant.438.clone) | copy-start | bytes 1540
  0.0 11.7 %copy-start.6 = (s32[128]{0:T(128)S(1)}, s32[128]{0:T(128)}, u32[]{:S(2)}) copy-start(s32[128]{0:T(128)} %constant.437.clone) | copy-start | bytes 1540
  0.0 11.6 %copy-start.5 = (s32[3,4]{1,0:T(4,128)S(1)}, s32[3,4]{1,0:T(4,128)}, u32[]{:S(2)}) copy-start(s32[3,4]{1,0:T(4,128)} %param.6) | copy-start | bytes 148
  0.0 14.1 %collective-permute-start.5 = (s32[3,4]{1,0:T(4,128)}, s32[3,4]{1,0:T(4,128)S(1)}, u32[]{:S(2)}, u32[]{:S(2)}) collective-permute-start(s32[3,4]{1,0:T(4,128)} %param.6), channel_id=1, source_target_pairs={{0,8},{8,16},{16,24},{24,0},{1,9},{9,17},{17,25},{25,1},{2,10},{10... | collective-permute-start | bytes 152 | tf_op jit(solution)/shard_map/ppermute | solution.py:18
  3.0 13.3 %collective-permute-start.7 = (s32[3,4]{1,0:T(4,128)}, s32[3,4]{1,0:T(4,128)S(1)}, u32[]{:S(2)}, u32[]{:S(2)}) collective-permute-start(s32[3,4]{1,0:T(4,128)} %param.6), channel_id=1, source_target_pairs={{0,24},{8,0},{16,8},{24,16},{1,25},{9,1},{17,9},{25,17},{2,26},{10... | collective-permute-start | bytes 152 | tf_op jit(solution)/shard_map/ppermute | solution.py:18
  4.1 12.3 %collective-permute-start.6 = (s32[3,4]{1,0:T(4,128)}, s32[3,4]{1,0:T(4,128)S(1)}, u32[]{:S(2)}, u32[]{:S(2)}) collective-permute-start(s32[3,4]{1,0:T(4,128)} %param.6), channel_id=1, source_target_pairs={{0,16},{8,24},{16,0},{24,8},{1,17},{9,25},{17,1},{25,9},{2,18},{10... | collective-permute-start | bytes 152 | tf_op jit(solution)/shard_map/ppermute | solution.py:18
  6.0 40.2 %collective-permute-start = (f32[3,20,60,128]{3,2,1,0:T(8,128)}, f32[3,20,60,128]{3,2,1,0:T(8,128)}, u32[]{:S(2)}, u32[]{:S(2)}) collective-permute-start(f32[3,20,60,128]{3,2,1,0:T(8,128)} %bitcast.66), channel_id=1, source_target_pairs={{0,4},{4,0},{1,5},{5,1},{2,6},{6,2},{3,7},{7,3},{8,12},{12,8},{9,1... | collective-permute-start | bytes 5529608 | tf_op jit(solution)/shard_map/ppermute | solution.py:18
  10.0 19.7 %collective-permute-start.1 = (f32[20,60,128]{2,1,0:T(8,128)}, f32[20,60,128]{2,1,0:T(8,128)S(1)}, u32[]{:S(2)}, u32[]{:S(2)}) collective-permute-start(f32[20,60,128]{2,1,0:T(8,128)} %get-tuple-element.7), channel_id=1, source_target_pairs={{0,1},{1,2},{2,3},{3,0},{4,5},{5,6},{6,7},{7,4},{8,9},{9,10},{10,1... | collective-permute-start | bytes 1843208 | tf_op jit(solution)/shard_map/ppermute | solution.py:18
  14.1 29.2 %collective-permute-start.3 = (f32[20,60,128]{2,1,0:T(8,128)}, f32[20,60,128]{2,1,0:T(8,128)S(1)}, u32[]{:S(2)}, u32[]{:S(2)}) collective-permute-start(f32[20,60,128]{2,1,0:T(8,128)} %get-tuple-element.8), channel_id=1, source_target_pairs={{0,3},{1,0},{2,1},{3,2},{4,7},{5,4},{6,5},{7,6},{8,11},{9,8},{10,9... | collective-permute-start | bytes 1843208 | tf_op jit(solution)/shard_map/ppermute | solution.py:18
  29.6 14.8 %copy-start.1 = (f32[20,60,128]{2,1,0:T(8,128)}, f32[20,60,128]{2,1,0:T(8,128)S(1)}, u32[]{:S(2)}) copy-start(f32[20,60,128]{2,1,0:T(8,128)S(1)} %collective-permute-done.1.refs_2_) | copy-start | bytes 1843204
  29.6 14.8 %collective-permute-start.2 = (f32[20,60,128]{2,1,0:T(8,128)S(1)}, f32[20,60,128]{2,1,0:T(8,128)S(1)}, u32[]{:S(2)}, u32[]{:S(2)}) collective-permute-start(f32[20,60,128]{2,1,0:T(8,128)S(1)} %collective-permute-done.1.refs_2_), channel_id=1, source_target_pairs={{0,4},{4,0},{1,5},{5,1},{2,6},{6,2},{3,7},{7,3},{8,12},{12,8},{9,1... | collective-permute-start | bytes 1843208 | tf_op jit(solution)/shard_map/ppermute | solution.py:18
  43.2 1.2 copy-start.2
  43.2 2.1 %collective-permute-start.4 = (f32[20,60,128]{2,1,0:T(8,128)S(1)}, f32[20,60,128]{2,1,0:T(8,128)S(1)}, u32[]{:S(2)}, u32[]{:S(2)}) collective-permute-start(f32[20,60,128]{2,1,0:T(8,128)S(1)} %collective-permute-done.3.refs_4_), channel_id=1, source_target_pairs={{0,4},{4,0},{1,5},{5,1},{2,6},{6,2},{3,7},{7,3},{8,12},{12,8},{9,1... | collective-permute-start | bytes 1843208 | tf_op jit(solution)/shard_map/ppermute | solution.py:18
  44.5 0.9 copy-start.3
  45.3 0.8 copy-start.4
  53.3 3.2 %copy-start = (bf16[3,20,256,256]{3,2,1,0:T(8,128)(2,1)S(1)}, bf16[3,20,256,256]{3,2,1,0:T(8,128)(2,1)}, u32[]{:S(2)}) copy-start(bf16[3,20,256,256]{3,2,1,0:T(8,128)(2,1)} %build_slabs.1) | copy-start | bytes 23592964
  67.8 36.9 %collective-permute-start.8 = (f32[128,2304]{1,0:T(8,128)S(1)}, f32[128,2304]{1,0:T(8,128)S(1)}, u32[]{:S(2)}, u32[]{:S(2)}) collective-permute-start(f32[128,2304]{1,0:T(8,128)S(1)} %contract_yz.5), channel_id=1, source_target_pairs={{0,16},{8,24},{16,0},{24,8},{1,17},{9,25},{17,1},{25,9},{2,18},{10... | collective-permute-start | bytes 3538952 | tf_op jit(solution)/shard_map/ppermute | solution.py:18
  79.6 28.9 %collective-permute-start.9 = (f32[128,2304]{1,0:T(8,128)S(1)}, f32[128,2304]{1,0:T(8,128)S(1)}, u32[]{:S(2)}, u32[]{:S(2)}) collective-permute-start(f32[128,2304]{1,0:T(8,128)S(1)} %contract_yz.6), channel_id=1, source_target_pairs={{0,24},{8,0},{16,8},{24,16},{1,25},{9,1},{17,9},{25,17},{2,26},{10... | collective-permute-start | bytes 3538952 | tf_op jit(solution)/shard_map/ppermute | solution.py:18
  92.5 41.5 %collective-permute-start.10 = (f32[128,2304]{1,0:T(8,128)S(1)}, f32[128,2304]{1,0:T(8,128)S(1)}, u32[]{:S(2)}, u32[]{:S(2)}) collective-permute-start(f32[128,2304]{1,0:T(8,128)S(1)} %contract_yz.7), channel_id=1, source_target_pairs={{0,8},{8,16},{16,24},{24,0},{1,9},{9,17},{17,25},{25,1},{2,10},{10... | collective-permute-start | bytes 3538952 | tf_op jit(solution)/shard_map/ppermute | solution.py:18
